TPU v7x, 256 devices: a whole 4x4x8 slice. The times are simulated.
256 devices in a mesh: shard: 16 (over z, core), tp: 4 (over y), shift: 4 (over x).
Axes of the slice: x: 4, y: 4, z: 8, core: 2. Of those that a mesh axis runs over, the one named last changes fastest.
Arguments:
- weight_query: bfloat16 [10240, 4096], P(('shift', 'shard'), 'tp'), parts along dimension 0, may hold values from -0.15625 to 0.15625
- low_query: bfloat16 [10240, 64], P(('shift', 'shard')), parts along dimension 0, may hold values from -0.125 to 0.125
- high_query: bfloat16 [256, 4096], P('shift', 'tp'), parts along dimension 0, may hold values from -0.75 to 0.75
- weight_key: bfloat16 [10240, 1024], P(('shift', 'shard'), 'tp'), parts along dimension 0, may hold values from -0.15625 to 0.15625
- low_key: bfloat16 [10240, 64], P(('shift', 'shard')), parts along dimension 0, may hold values from -0.125 to 0.125
- high_key: bfloat16 [256, 1024], P('shift', 'tp'), parts along dimension 0, may hold values from -0.75 to 0.75
- weight_value: bfloat16 [10240, 1024], P(('shift', 'shard'), 'tp'), parts along dimension 0, may hold values from -0.15625 to 0.15625
- low_value: bfloat16 [10240, 64], P(('shift', 'shard')), parts along dimension 0, may hold values from -0.125 to 0.125
- high_value: bfloat16 [256, 1024], P('shift', 'tp'), parts along dimension 0, may hold values from -0.75 to 0.75
- norm_train: float32 [10240], P(('shift', 'shard', 'tp')), parts along dimension 0, may hold values from 0.25 to 1.75
- norm_step: float32 [10240], P(('shift', 'shard', 'tp')), parts along dimension 0, may hold values from -0.3 to 0.3
Outputs:
- serve_query: bfloat16 [10240, 4096], P('shift', 'tp'), parts along dimension 0
- serve_key: bfloat16 [10240, 1024], P('shift', 'tp'), parts along dimension 0
- serve_value: bfloat16 [10240, 1024], P('shift', 'tp'), parts along dimension 0
- factor_query: float32 [16384], P(('shift', 'tp')), parts along dimension 0
- factor_key: float32 [4096], P(('shift', 'tp')), parts along dimension 0
- factor_value: float32 [4096], P(('shift', 'tp')), parts along dimension 0
- serve_norm: bfloat16 [10240], P('shift'), parts along dimension 0
There are 4 independent parts, one for each index of `shift`. A program takes and returns all parts, laid end to end along the dimension named above; each array names one. Nothing has to cross between parts.
All inputs are finite; a program needn't handle non-finite values. Where the computation divides by a largest or mean magnitude, that divisor is 1e-20 or more.
Results may differ from a plain program's by a relative error of at most 0.001.
Values may be sent and summed in bfloat16 or wider, within the bound.
A program may use at most 64 MiB of HBM per device.

v0:
```python
import jax
import jax.numpy as jnp
from jax import lax
from jax.sharding import PartitionSpec as P

D_MODEL = 2560


mix_rate = 1.0


def from_everyone(x, axis):
    copies = jnp.broadcast_to(x, (lax.axis_size(axis), *x.shape))
    return lax.all_to_all(copies, axis, split_axis=0, concat_axis=0, tiled=True)


def over_copies(x, axis):
    everything = from_everyone(x, axis)
    return jnp.sum(everything, axis=0)


def in_one(arrays, axis):
    ends = [0]
    for a in arrays:
        ends.append(ends[-1] + a.size)
    so_far = over_copies(jnp.concatenate([a.ravel() for a in arrays]), axis)
    return tuple((so_far[b:e].reshape(a.shape) for a, b, e in zip(arrays, ends, ends[1:])))


def side_by_side(arrays, axis, dim, along):
    both = jnp.concatenate(arrays, axis=along)
    result, at, done = (lax.all_gather(both, axis, axis=dim, tiled=True), 0, [])
    for a in arrays:
        done.append(lax.slice_in_dim(result, at, at + a.shape[along], axis=along))
        at += a.shape[along]
    return tuple(done)


def in_order(pieces, dim):
    dims = list(pieces.shape[1:])
    dims[dim] *= pieces.shape[0]
    return jnp.moveaxis(pieces, 0, dim).reshape(dims)


def gather_directly(x, axis, dim):
    return in_order(from_everyone(x, axis), dim)


def per_device(
    weight_query,
    low_query,
    high_query,
    weight_key,
    low_key,
    high_key,
    weight_value,
    low_value,
    high_value,
    norm_train,
    norm_step,
):
    fresh_query = weight_query.astype(jnp.float32) + mix_rate * jnp.dot(
        low_query, high_query, preferred_element_type=jnp.float32
    )
    fresh_key = weight_key.astype(jnp.float32) + mix_rate * jnp.dot(
        low_key, high_key, preferred_element_type=jnp.float32
    )
    fresh_value = weight_value.astype(jnp.float32) + mix_rate * jnp.dot(
        low_value, high_value, preferred_element_type=jnp.float32
    )
    total_query, total_key, total_value = in_one(
        (
            jnp.sum(jnp.abs(fresh_query), axis=0),
            jnp.sum(jnp.abs(fresh_key), axis=0),
            jnp.sum(jnp.abs(fresh_value), axis=0),
        ),
        "shard",
    )
    factor_query = total_query / D_MODEL
    factor_key = total_key / D_MODEL
    factor_value = total_value / D_MODEL
    narrow_query, narrow_key, narrow_value = (
        (fresh_query / factor_query).astype(jnp.bfloat16),
        (fresh_key / factor_key).astype(jnp.bfloat16),
        (fresh_value / factor_value).astype(jnp.bfloat16),
    )
    serve_query, serve_key, serve_value = side_by_side(
        (narrow_query, narrow_key, narrow_value), "shard", 0, 1
    )
    serve_norm = gather_directly((norm_train + norm_step).astype(jnp.bfloat16), ("shard", "tp"), 0)
    return (serve_query, serve_key, serve_value, factor_query, factor_key, factor_value, serve_norm)


def solution(mesh):
    return jax.shard_map(
        per_device,
        mesh=mesh,
        in_specs=(
            P(("shift", "shard"), "tp"),
            P(("shift", "shard"), None),
            P("shift", "tp"),
            P(("shift", "shard"), "tp"),
            P(("shift", "shard"), None),
            P("shift", "tp"),
            P(("shift", "shard"), "tp"),
            P(("shift", "shard"), None),
            P("shift", "tp"),
            P(("shift", "shard", "tp")),
            P(("shift", "shard", "tp")),
        ),
        out_specs=(
            P("shift", "tp"),
            P("shift", "tp"),
            P("shift", "tp"),
            P(("shift", "tp")),
            P(("shift", "tp")),
            P(("shift", "tp")),
            P("shift"),
        ),
        check_vma=False,
    )
```

profile of v0, /device:TPU:1, one launch (start us, length us, event | category | flops | bytes accessed | tf_op | source)
XLA Modules:
  0.0 96.3 jit_solution(13001443479749766300)
XLA Ops:
  7.2 0.0 copy-start
  7.2 0.0 copy-start.1
  7.2 0.0 copy-start.2
  7.2 0.0 copy-start.3
  7.2 0.0 all-gather.2.cloned.1.call-start
  7.3 0.8 copy-done
  8.1 1.3 %abs_reduce_fusion = (f32[1024]{0:T(1024)S(1)}, f32[160,1024]{1,0:T(8,128)S(1)}) fusion(bf16[160,64]{0,1:T(8,128)(2,1)} %param.12, bf16[64,1024]{1,0:T(8,128)(2,1)S(1)} %copy-done, bf16[160,1024]{1,0:T(8,128)(2,1)} %param.11), kind=kOutput, calls=%fused_computation.4 | convolution fusion | flops 21625856 | bytes 1138688 | tf_op jit(solution)/shard_map/dot_general | solution.py:62
  9.4 1.1 %abs_reduce_fusion.1 = (f32[256]{0:T(256)S(1)}, f32[160,256]{1,0:T(8,128)S(1)}) fusion(bf16[160,64]{0,1:T(8,128)(2,1)} %param.18, bf16[64,256]{1,0:T(8,128)(2,1)} %param.19, bf16[160,256]{1,0:T(8,128)(2,1)} %param.17), kind=kOutput, calls=%fused_computation.8 | convolution fusion | flops 5406464 | bytes 300032 | tf_op jit(solution)/shard_map/dot_general | solution.py:68
  10.5 0.0 copy-done.1
  10.5 0.0 copy-done.2
  10.5 0.0 copy-done.3
  10.5 0.2 abs_reduce_fusion.2
  10.8 0.1 broadcast_in_dim.4
  10.8 18.2 %all_to_all.12 = f32[16,1,1536]{2,1,0:T(1,128)S(1)} all-to-all(f32[16,1,1536]{2,1,0:T(1,128)S(1)} %broadcast_in_dim.4), channel_id=1, replica_groups=mesh['shard'=16,'tp'=4,'shift'=4] {'shard'}, dimensions={0} | all-to-all | bytes 196608 | tf_op jit(solution)/shard_map/all_to_all | solution.py:14
  29.1 0.1 reduce_sum.39
  29.1 0.0 copy-start.5
  29.1 0.0 copy-start.6
  29.2 0.0 copy-start.4
  29.2 0.0 copy-start.7
  29.2 0.0 copy-start.8
  29.2 0.1 divide_convert_fusion
  29.3 0.8 pad_maximum_fusion
  30.1 0.0 all-gather.2.cloned.1.call-update
  30.2 0.0 copy-done.5
  30.2 0.0 copy-done.6
  30.2 0.0 copy-done.4
  30.2 0.0 copy-done.7
  30.2 0.0 copy-done.8
  30.2 14.8 %all_to_all.13 = bf16[64,1,40]{2,1,0:T(2,128)(2,1)S(1)} all-to-all(bf16[64,1,40]{2,1,0:T(2,128)(2,1)S(1)} %broadcast_in_dim.10), channel_id=1, replica_groups=mesh['shard'=16,'tp'=4,'shift'=4] {'shard','tp'}, dimensions={0} | all-to-all | bytes 10240 | tf_op jit(solution)/shard_map/all_to_all | solution.py:14
  45.0 0.1 reduce.1
  45.1 0.7 reshape.29
  45.8 34.8 %all-gather.2.cloned.1.call-done = bf16[2560,1536]{1,0:T(8,128)(2,1)} async-done(((bf16[160,1536]{1,0:T(8,128)(2,1)}), bf16[2560,1536]{1,0:T(8,128)(2,1)}) %all-gather.2.cloned.1.call-update) | async-done | bytes 7864336 | tf_op jit(solution)/shard_map/all_gather | solution.py:32
  80.6 3.4 %fusion = (bf16[2560,256]{1,0:T(8,128)(2,1)}, bf16[2560,256]{1,0:T(8,128)(2,1)}) fusion(bf16[2560,1536]{1,0:T(8,128)(2,1)} %all-gather.2.cloned.1.call-done), kind=kLoop, calls=%fused_computation.15 | loop fusion | bytes 5242880 | tf_op jit(solution)/shard_map/slice | solution.py:34
  84.0 5.4 %slice.27 = bf16[2560,1024]{1,0:T(8,128)(2,1)} slice(bf16[2560,1536]{1,0:T(8,128)(2,1)} %all-gather.2.cloned.1.call-done), slice={[0:2560], [0:1024]} | slice | bytes 10485760 | tf_op jit(solution)/shard_map/slice | solution.py:34
  (6 shorter events, 0.1 us)
Async XLA Ops:
  7.2 0.9 copy-start
  7.2 3.3 %copy-start.1 = (bf16[160,256]{1,0:T(8,128)(2,1)S(1)}, bf16[160,256]{1,0:T(8,128)(2,1)}, u32[]{:S(2)}) copy-start(bf16[160,256]{1,0:T(8,128)(2,1)} %param.14) | copy-start | bytes 245764
  7.2 3.3 %copy-start.2 = (bf16[160,64]{0,1:T(8,128)(2,1)S(1)}, bf16[160,64]{0,1:T(8,128)(2,1)}, u32[]{:S(2)}) copy-start(bf16[160,64]{0,1:T(8,128)(2,1)} %param.15) | copy-start | bytes 61444
  7.2 3.3 %copy-start.3 = (bf16[64,256]{1,0:T(8,128)(2,1)S(1)}, bf16[64,256]{1,0:T(8,128)(2,1)}, u32[]{:S(2)}) copy-start(bf16[64,256]{1,0:T(8,128)(2,1)} %param.16) | copy-start | bytes 98308
  7.2 73.4 %all-gather.2.cloned.1.call-start = ((), (), s32[]{:S(2)}) async-start(), calls=%async_computation.2 | async-start | bytes 8355840 | tf_op jit(solution)/shard_map/all_gather | solution.py:32
  29.1 1.0 %copy-start.5 = (f32[256]{0:T(256)}, f32[256]{0:T(256)S(1)}, u32[]{:S(2)}) copy-start(f32[256]{0:T(256)S(1)} %get-tuple-element.9) | copy-start | bytes 3076
  29.1 1.0 %copy-start.6 = (f32[256]{0:T(256)}, f32[256]{0:T(256)S(1)}, u32[]{:S(2)}) copy-start(f32[256]{0:T(256)S(1)} %get-tuple-element.10) | copy-start | bytes 3076
  29.2 1.0 %copy-start.4 = (f32[1024]{0:T(1024)}, f32[1024]{0:T(1024)S(1)}, u32[]{:S(2)}) copy-start(f32[1024]{0:T(1024)S(1)} %slice_multiply_fusion) | copy-start | bytes 12292
  29.2 1.0 %copy-start.7 = (f32[40]{0:T(128)S(1)}, f32[40]{0:T(128)}, u32[]{:S(2)}) copy-start(f32[40]{0:T(128)} %param.20) | copy-start | bytes 484
  29.2 1.0 %copy-start.8 = (f32[40]{0:T(128)S(1)}, f32[40]{0:T(128)}, u32[]{:S(2)}) copy-start(f32[40]{0:T(128)} %param.21) | copy-start | bytes 484
Sparse Core Ops, SparseCore 0:
  30.3 50.3 all-gather.1
where the time goes:
time: 96.6 us; the launch traced here: 96.3 us
  waiting for transfers between devices  34.8 us (36%)
  blocking collectives  33 us (34%)
  between operations  14.2 us (15%)
  local copies, waits for them, and re-layouts  10.4 us (11%)
  matrix products  2.63 us (3%)
  other arithmetic  1.09 us (1%)
    all_gather x1, waiting for transfers between devices, side_by_side(): result, at, done = (lax.all_gather(both, axis, axis=dim, tiled=True), 0, [])  34.8 us
    all_to_all x2, blocking collectives, from_everyone(): return lax.all_to_all(copies, axis, split_axis=0, concat_axis=0, tiled=True)  33 us
    slice x2, local copies, waits for them, and re-layouts, side_by_side(): done.append(lax.slice_in_dim(result, at, at + a.shape[along], axis=along))  8.8 us
  transfers between devices with their start and end apart: 1, of which 1 were waited for; matrix products, arithmetic and copies ran while one was open for 1% of the time, Pallas kernels for 0%

commit v1 on v0

v1 whole, which is shorter than its diff:
```python
import functools

import jax
import jax.numpy as jnp
from jax import lax
from jax.experimental import pallas as pl
from jax.experimental.pallas import tpu as pltpu
from jax.sharding import PartitionSpec as P

MESH = pl.DeviceIdType.MESH
F32 = jnp.float32
BF16 = jnp.bfloat16

mix_rate = 1.0

CHUNKS = ((1, 0, 160), (2, 0, 160), (0, 0, 48), (0, 48, 64), (0, 112, 48))
LAST = ((0, 1, 2), (3, 4))
COLS = (0, 1024, 1280, 1536)
TILE = 256


def kernel(
    wq, lq, hq, wk, lk, hk, wv, lv, hv, nt, ns,
    oq, ok, ov, fq, fk, fv, on,
    sw0, sw1, sw2, sl0, sl1, sl2, sh0, sh1, sh2, snt, sns,
    rw0, rw1, rw2, rl0, rl1, rl2, prod,
    st, stp, msg, gath, fin, nrm, nall, inv, nout, nrow,
    load_sem, sr_send, sr_recv, st_send, st_recv, g_send, g_recv, f_send, f_recv,
    n_send, n_recv, y_send, y_recv, low_send, low_recv, r_send, r_recv, p_send, p_recv,
):
    shard = lax.axis_index("shard")
    y = lax.axis_index("tp")
    z, c = shard // 2, shard % 2
    nz = 8
    rows = wq.shape[0]
    d_model = rows * 16
    outs = (oq, ok, ov)
    w = (sw0, sw1, sw2)
    low = (sl0, sl1, sl2)
    high = (sh0, sh1, sh2)
    rw = (rw0, rw1, rw2)
    rl = (rl0, rl1, rl2)
    step = (1 - 2 * c, 2 * c - 1)

    def at(zz, cc):
        return {"shard": lax.rem(zz + 4 * nz, nz) * 2 + cc}

    partner = at(z, 1 - c)
    nbr = (at(z + step[0], c), at(z + step[1], c))

    loads = []
    for i, (src, dst) in enumerate(
        zip((wk, wv, wq, lq, lk, lv, hq, hk, hv, nt, ns), (sw1, sw2, sw0, sl0, sl1, sl2, sh0, sh1, sh2, snt, sns))
    ):
        cp = pltpu.make_async_copy(src, dst, load_sem.at[i])
        cp.start()
        loads.append(cp)

    barrier = pltpu.get_barrier_semaphore()
    peers = [at(z + d, c) for d in range(1, nz)] + [partner] + [{"tp": lax.rem(y + d, 4)} for d in range(1, 4)]
    for peer in peers:
        pl.semaphore_signal(barrier, inc=1, device_id=peer, device_id_type=MESH)
    for cp in loads:
        cp.wait()
    pl.semaphore_wait(barrier, len(peers))

    sends = []

    def send(src, dst, s_sem, r_sem, to):
        cp = pltpu.make_async_remote_copy(
            src_ref=src, dst_ref=dst, send_sem=s_sem, recv_sem=r_sem, device_id=to, device_id_type=MESH
        )
        cp.start()
        sends.append(cp)

    def arrived(dst, sem):
        pltpu.make_async_remote_copy(
            src_ref=dst, dst_ref=dst, send_sem=sem, recv_sem=sem, device_id=partner, device_id_type=MESH
        ).wait_recv()

    def send_raw(i):
        a, r0, n = CHUNKS[i]
        for d in range(2):
            send(w[a].at[pl.ds(r0, n)], rw[a].at[d, pl.ds(r0, n)], r_send.at[d, 0, i], r_recv.at[d, 0, i], nbr[d])

    send_raw(0)

    def product(l_ref, h_ref, out, a):
        for t in range(0, COLS[a + 1] - COLS[a], TILE):
            out[:, COLS[a] + t : COLS[a] + t + TILE] = mix_rate * lax.dot_general(
                l_ref[...], h_ref[:, t : t + TILE], (((0,), (0,)), ((), ())), preferred_element_type=F32
            )

    for a in range(3):
        product(low[a], high[a], prod.at[2], a)
    st[...] = jnp.zeros_like(st)
    for a in range(3):
        for t in range(0, COLS[a + 1] - COLS[a], TILE):
            col = COLS[a] + t
            fresh = w[a][:, t : t + TILE].astype(F32) + prod[2, :, col : col + TILE]
            prod[2, :, col : col + TILE] = fresh
            total = jnp.sum(jnp.abs(fresh), axis=0, keepdims=True)
            for g in range(TILE // 128):
                j = col // 128 + g
                st[j // 6, j % 6 : j % 6 + 1, :] = total[:, 128 * g : 128 * (g + 1)]

    send(st.at[1 - c], stp, sr_send, sr_recv, partner)
    arrived(stp, sr_recv)
    msg[0:6, :] = st[c, 0:6, :] + stp[0:6, :]
    msg[6:8, :] = jnp.zeros((2, 128), F32)
    msg[6:7, 0:40] = (snt[...] + sns[...]).reshape(1, 40)
    gath[z] = msg[...]
    for d in range(1, nz):
        send(msg, gath.at[z], g_send.at[d - 1], g_recv.at[d - 1], at(z + d, c))
    for d in range(2):
        for a in range(3):
            send(low[a], rl[a].at[d], low_send.at[d, a], low_recv.at[d, a], nbr[d])
    for i in range(1, len(CHUNKS)):
        send_raw(i)

    for d in range(1, nz):
        arrived(gath.at[lax.rem(z - d + nz, nz)], g_recv.at[d - 1])
    total = gath[0]
    for k in range(1, nz):
        total = total + gath[k]
    fin[c] = total * (1.0 / d_model)
    for k in range(nz):
        nrm[c, k : k + 1, :] = gath[k, 6:7, :]
    send(fin.at[c], fin.at[c], f_send, f_recv, partner)
    send(nrm.at[c], nrm.at[c], n_send, n_recv, partner)
    arrived(fin.at[1 - c], f_recv)
    for j in range(12):
        row = fin[j // 6, j % 6 : j % 6 + 1, :]
        inv[:, 128 * j : 128 * (j + 1)] = 1.0 / row
        if j < 8:
            fq[:, 128 * j : 128 * (j + 1)] = row
        elif j < 10:
            fk[:, 128 * (j - 8) : 128 * (j - 7)] = row
        else:
            fv[:, 128 * (j - 10) : 128 * (j - 9)] = row

    def place(a, zz, cc, r0, n):
        first = pl.multiple_of((lax.rem(zz + 4 * nz, nz) * 2 + cc) * rows, 16)
        return outs[a].at[pl.ds(first + r0, n)]

    def origin(d, h):
        return z - h * step[d]

    for i, (a, r0, n) in enumerate(CHUNKS):
        dst = place(a, z, c, r0, n)
        for t in range(0, COLS[a + 1] - COLS[a], TILE):
            col = COLS[a] + t
            dst[:, t : t + TILE] = (prod[2, r0 : r0 + n, col : col + TILE] * inv[:, col : col + TILE]).astype(BF16)
        send(dst, dst, p_send.at[0, 0, i], p_recv.at[0, 0, i], partner)

    for d in range(2):
        for a in range(3):
            arrived(rl[a].at[d], low_recv.at[d, a])
            product(rl[a].at[d], high[a], prod.at[d], a)
    for i, (a, r0, n) in enumerate(CHUNKS):
        for d in range(2):
            arrived(rw[a].at[d, pl.ds(r0, n)], r_recv.at[d, 0, i])
            dst = place(a, origin(d, 1), c, r0, n)
            for t in range(0, COLS[a + 1] - COLS[a], TILE):
                col = COLS[a] + t
                fresh = rw[a][d, r0 : r0 + n, t : t + TILE].astype(F32) + prod[d, r0 : r0 + n, col : col + TILE]
                dst[:, t : t + TILE] = (fresh * inv[:, col : col + TILE]).astype(BF16)
            send(dst, dst, r_send.at[d, 1, i], r_recv.at[d, 1, i], nbr[d])
            send(dst, dst, p_send.at[d, 1, i], p_recv.at[d, 1, i], partner)

    arrived(nrm.at[1 - c], n_recv)
    nall[y] = nrm[...]
    for d in range(1, 4):
        send(nrm, nall.at[y], y_send.at[d - 1], y_recv.at[d - 1], {"tp": lax.rem(y + d, 4)})

    for h in (2, 3, 4):
        for i, (a, r0, n) in enumerate(CHUNKS):
            for d in range(2):
                if h == 4 and i not in LAST[d]:
                    continue
                dst = place(a, origin(d, h), c, r0, n)
                arrived(dst, r_recv.at[d, h - 1, i])
                if h == 2 or (h == 3 and i in LAST[d]):
                    send(dst, dst, r_send.at[d, h, i], r_recv.at[d, h, i], nbr[d])
                send(dst, dst, p_send.at[d, h, i], p_recv.at[d, h, i], partner)
        if h == 2:
            for d in range(1, 4):
                arrived(nall.at[lax.rem(y - d + 4, 4)], y_recv.at[d - 1])
            for b in range(4):
                for yy in range(4):
                    k = 4 * b + yy
                    for g in range(4):
                        s = 4 * g + b
                        nout[g : g + 1, 40 * k : 40 * k + 40] = nall[yy, s % 2, s // 2 : s // 2 + 1, 0:40]
            for g in range(4):
                for j in range(5):
                    nrow[5 * g + j : 5 * g + j + 1, :] = nout[g : g + 1, 128 * j : 128 * (j + 1)]
            on[...] = nrow[...].astype(BF16)

    for i, (a, r0, n) in enumerate(CHUNKS):
        arrived(place(a, z, 1 - c, r0, n), p_recv.at[0, 0, i])
    for h in (1, 2, 3, 4):
        for i, (a, r0, n) in enumerate(CHUNKS):
            for d in range(2):
                if h == 4 and i not in LAST[d]:
                    continue
                arrived(place(a, z + h * step[d], 1 - c, r0, n), p_recv.at[d, h, i])
    for cp in sends:
        cp.wait_send()


def flush(*refs):
    sem = refs[-1]
    copies = [pltpu.make_async_copy(refs[i], refs[7 + i], sem.at[i]) for i in range(7)]
    for cp in copies:
        cp.start()
    for cp in copies:
        cp.wait()


def per_device(wq, lq, hq, wk, lk, hk, wv, lv, hv, nt, ns):
    rows = wq.shape[0]
    n = len(CHUNKS)
    dma = pltpu.SemaphoreType.DMA
    any_spec = pl.BlockSpec(memory_space=pltpu.HBM)
    vm = pl.BlockSpec(memory_space=pltpu.VMEM)
    widths = (wq.shape[1], wk.shape[1], wv.shape[1])
    rank = hq.shape[0]
    wide = sum(widths)
    out_shape = (
        *(pltpu.VMEM((16 * rows, m), BF16) for m in widths),
        *(pltpu.VMEM((1, m), F32) for m in widths),
        pltpu.VMEM((20, 128), BF16),
    )
    scratch = (
        *(pltpu.VMEM((rows, m), BF16) for m in widths),
        *(pltpu.VMEM((rank, rows), BF16) for _ in widths),
        *(pltpu.VMEM((rank, m), BF16) for m in widths),
        pltpu.VMEM((40,), F32),
        pltpu.VMEM((40,), F32),
        *(pltpu.VMEM((2, rows, m), BF16) for m in widths),
        *(pltpu.VMEM((2, rank, rows), BF16) for _ in widths),
        pltpu.VMEM((3, rows, wide), F32),
        pltpu.VMEM((2, 8, 128), F32),
        pltpu.VMEM((8, 128), F32),
        pltpu.VMEM((8, 128), F32),
        pltpu.VMEM((8, 8, 128), F32),
        pltpu.VMEM((2, 8, 128), F32),
        pltpu.VMEM((2, 8, 128), F32),
        pltpu.VMEM((4, 2, 8, 128), F32),
        pltpu.VMEM((1, wide), F32),
        pltpu.VMEM((4, 640), F32),
        pltpu.VMEM((20, 128), F32),
        dma((11,)),
        dma, dma, dma, dma,
        dma((7,)), dma((7,)),
        dma, dma, dma, dma,
        dma((3,)), dma((3,)),
        dma((2, 3)), dma((2, 3)),
        dma((2, 4, n)), dma((2, 4, n)),
        dma((2, 5, n)), dma((2, 5, n)),
    )
    oq, ok, ov, fq, fk, fv, on = pl.pallas_call(
        kernel,
        out_shape=out_shape,
        in_specs=[any_spec] * 11,
        out_specs=(vm,) * 7,
        scratch_shapes=scratch,
        compiler_params=pltpu.CompilerParams(
            collective_id=0, has_side_effects=True, vmem_limit_bytes=24 * 1024 * 1024
        ),
    )(*(pltpu.with_memory_space_constraint(a, pltpu.HBM) for a in (wq, lq.T, hq, wk, lk.T, hk, wv, lv.T, hv, nt, ns)))
    made = (oq, ok, ov, fq, fk, fv, on)
    oq, ok, ov, fq, fk, fv, on = pl.pallas_call(
        flush,
        out_shape=tuple(jax.ShapeDtypeStruct(a.shape, a.dtype) for a in made),
        in_specs=[vm] * 7,
        out_specs=(pl.BlockSpec(memory_space=pltpu.HBM),) * 7,
        scratch_shapes=(dma((7,)),),
        compiler_params=pltpu.CompilerParams(vmem_limit_bytes=1024 * 1024),
    )(*(pltpu.with_memory_space_constraint(a, pltpu.VMEM) for a in made))
    return oq, ok, ov, fq.reshape(-1), fk.reshape(-1), fv.reshape(-1), on.reshape(-1)


def solution(mesh):
    return jax.shard_map(
        per_device,
        mesh=mesh,
        in_specs=(
            P(("shift", "shard"), "tp"),
            P(("shift", "shard"), None),
            P("shift", "tp"),
            P(("shift", "shard"), "tp"),
            P(("shift", "shard"), None),
            P("shift", "tp"),
            P(("shift", "shard"), "tp"),
            P(("shift", "shard"), None),
            P("shift", "tp"),
            P(("shift", "shard", "tp")),
            P(("shift", "shard", "tp")),
        ),
        out_specs=(
            P("shift", "tp"),
            P("shift", "tp"),
            P("shift", "tp"),
            P(("shift", "tp")),
            P(("shift", "tp")),
            P(("shift", "tp")),
            P("shift"),
        ),
        check_vma=False,
    )
```

time: 96.6 us -> 58.5 us (0.61)
  Pallas kernels: 0 us -> 57.7 us
  waiting for transfers between devices: 34.8 us -> 0 us
  blocking collectives: 33 us -> 0 us
  between operations: 14.2 us -> 0.64 us
  local copies, waits for them, and re-layouts: 10.4 us -> 0 us
  matrix products: 2.63 us -> 0 us
  other arithmetic: 1.09 us -> 0 us
    pallas_call x0 -> x2, Pallas kernels: none -> 57.7 us  [the longest x1 54.5 us: per_device(): pl.pallas_call(kernel, out_shape=out_shape, in_specs=[any_spec] * 11, out...]
    all_gather x1 -> x0, waiting for transfers between devices: 34.8 us -> none  [side_by_side(): result, at, done = (lax.all_gather(both, axis, axis=dim, tiled=True), 0, [])]
    all_to_all x2 -> x0, blocking collectives: 33 us -> none  [from_everyone(): return lax.all_to_all(copies, axis, split_axis=0, concat_axis=0, tiled=True)]
    slice x2 -> x0, local copies, waits for them, and re-layouts: 8.8 us -> none  [side_by_side(): done.append(lax.slice_in_dim(result, at, at + a.shape[along], axis=along))]
    dot_general x3 -> x0, matrix products: 2.63 us -> none  [the longest x1 1.27 us: per_device(): jnp.dot(low_query, high_query, preferred_element_type=jnp.float32)]
  transfers between devices with their start and end apart: 1 -> 0, of which waited for: 1 -> 0; matrix products, arithmetic and copies ran while one was open for 1% -> 0% of each run, Pallas kernels for 0% -> 0%
where the time goes in v1:
time: 58.5 us; the launch traced here: 58.4 us
  Pallas kernels  57.7 us (99%)
  between operations  0.64 us (1%)
    pallas_call x1, Pallas kernels, per_device(): pl.pallas_call(kernel, out_shape=out_shape, in_specs=[any_spec] * 11, out...  54.5 us
    pallas_call x1, Pallas kernels, per_device(): pl.pallas_call(flush, out_shape=tuple((jax.ShapeDtypeStruct(a.shape, a.dt...  3.25 us

profile of v1, /device:TPU:1, one launch (start us, length us, event | category | flops | bytes accessed | tf_op | source)
XLA Modules:
  0.0 58.4 jit_solution(9506112477698792216)
XLA Ops:
  0.6 54.5 %shard_map.162 = (bf16[2560,1024]{1,0:T(8,128)(2,1)S(1)}, bf16[2560,256]{1,0:T(8,128)(2,1)S(1)}, bf16[2560,256]{1,0:T(8,128)(2,1)S(1)}, f32[1,1024]{1,0:T(1,128)...) custom-call(bf16[160,1024]{1,0:T(8,128)(2,1)} %wq.1, bf16[64,160]{1,0:T(8,128)(2,1)} %bitcast.7, ...), custom_call_target="tpu_custom_call" | custom-call | tf_op jit(solution)/shard_map/pallas_call | solution.py:263
  55.1 3.2 %shard_map.163 = (bf16[2560,1024]{1,0:T(8,128)(2,1)}, bf16[2560,256]{1,0:T(8,128)(2,1)}, bf16[2560,256]{1,0:T(8,128)(2,1)}, f32[1,1024]{1,0:T(1,128)}, f32[1,256...) custom-call(bf16[2560,1024]{1,0:T(8,128)(2,1)S(1)} %get-tuple-element.21.refs_0_, ...), custom_call_target="tpu_custom_call" | custom-call | tf_op jit(solution)/shard_map/pallas_call | solution.py:274

commit v2 on v1

--- a/solution.py
+++ b/solution.py
@@ -22,47 +22,56 @@
 def kernel(
     wq, lq, hq, wk, lk, hk, wv, lv, hv, nt, ns,
     oq, ok, ov, fq, fk, fv, on,
-    sw0, sw1, sw2, sl0, sl1, sl2, sh0, sh1, sh2, snt, sns,
-    rw0, rw1, rw2, rl0, rl1, rl2, prod,
+    sw0, sw1, sw2, low, sh0, sh1, sh2, snt, sns,
+    rw0, rw1, rw2, rlow, prod,
     st, stp, msg, gath, fin, nrm, nall, inv, nout, nrow,
-    load_sem, sr_send, sr_recv, st_send, st_recv, g_send, g_recv, f_send, f_recv,
-    n_send, n_recv, y_send, y_recv, low_send, low_recv, r_send, r_recv, p_send, p_recv,
+    load_sem, far, sr_send, sr_recv, g_send, g_recv, f_send, f_recv,
+    n_send, n_recv, y_send, y_recv, low_send, low_recv, ly_send, ly_recv, r_send, r_recv, p_send, p_recv,
 ):
     shard = lax.axis_index("shard")
     y = lax.axis_index("tp")
     z, c = shard // 2, shard % 2
-    nz = 8
+    nz, ny = 8, 4
     rows = wq.shape[0]
     d_model = rows * 16
     outs = (oq, ok, ov)
     w = (sw0, sw1, sw2)
-    low = (sl0, sl1, sl2)
     high = (sh0, sh1, sh2)
     rw = (rw0, rw1, rw2)
-    rl = (rl0, rl1, rl2)
     step = (1 - 2 * c, 2 * c - 1)
 
     def at(zz, cc):
         return {"shard": lax.rem(zz + 4 * nz, nz) * 2 + cc}
 
+    def rank_of(d):
+        return {"tp": lax.rem(y + d, ny)}
+
     partner = at(z, 1 - c)
     nbr = (at(z + step[0], c), at(z + step[1], c))
 
-    loads = []
-    for i, (src, dst) in enumerate(
-        zip((wk, wv, wq, lq, lk, lv, hq, hk, hv, nt, ns), (sw1, sw2, sw0, sl0, sl1, sl2, sh0, sh1, sh2, snt, sns))
-    ):
-        cp = pltpu.make_async_copy(src, dst, load_sem.at[i])
+    pairs = (
+        (lq, low.at[0]), (lk, low.at[1]), (lv, low.at[2]), (wk, sw1), (wv, sw2),
+        (hk, sh1), (hv, sh2), (hq, sh0), (wq, sw0), (nt, snt), (ns, sns),
+    )
+    loads = [pltpu.make_async_copy(src, dst, load_sem.at[i]) for i, (src, dst) in enumerate(pairs)]
+    for cp in loads:
         cp.start()
-        loads.append(cp)
 
     barrier = pltpu.get_barrier_semaphore()
-    peers = [at(z + d, c) for d in range(1, nz)] + [partner] + [{"tp": lax.rem(y + d, 4)} for d in range(1, 4)]
+    peers = [*nbr, partner, *(rank_of(d) for d in range(1, ny))]
     for peer in peers:
         pl.semaphore_signal(barrier, inc=1, device_id=peer, device_id_type=MESH)
-    for cp in loads:
-        cp.wait()
     pl.semaphore_wait(barrier, len(peers))
+
+    def pass_on(k):
+        for d in range(2):
+            pl.semaphore_signal(far.at[d, k - 1], inc=1, device_id=nbr[d], device_id_type=MESH)
+
+    def heard(k):
+        for d in range(2):
+            pl.semaphore_wait(far.at[d, k - 1], 1)
+
+    pass_on(1)
 
     sends = []
 
@@ -83,7 +92,18 @@
         for d in range(2):
             send(w[a].at[pl.ds(r0, n)], rw[a].at[d, pl.ds(r0, n)], r_send.at[d, 0, i], r_recv.at[d, 0, i], nbr[d])
 
+    def quarter(rank):
+        share = low.shape[1] // ny
+        return pl.ds(pl.multiple_of(rank * share, share), share)
+
+    for i in range(3):
+        loads[i].wait()
+    for d in range(2):
+        send(low.at[:, quarter(y)], rlow.at[d, :, quarter(y)], low_send.at[d], low_recv.at[d], nbr[d])
+    loads[3].wait()
     send_raw(0)
+    loads[4].wait()
+    send_raw(1)
 
     def product(l_ref, h_ref, out, a):
         for t in range(0, COLS[a + 1] - COLS[a], TILE):
@@ -91,10 +111,11 @@
                 l_ref[...], h_ref[:, t : t + TILE], (((0,), (0,)), ((), ())), preferred_element_type=F32
             )
 
-    for a in range(3):
-        product(low[a], high[a], prod.at[2], a)
+    for i in range(5, 11):
+        loads[i].wait()
     st[...] = jnp.zeros_like(st)
-    for a in range(3):
+    for a in (1, 2, 0):
+        product(low.at[a], high[a], prod.at[2], a)
         for t in range(0, COLS[a + 1] - COLS[a], TILE):
             col = COLS[a] + t
             fresh = w[a][:, t : t + TILE].astype(F32) + prod[2, :, col : col + TILE]
@@ -105,18 +126,39 @@
                 st[j // 6, j % 6 : j % 6 + 1, :] = total[:, 128 * g : 128 * (g + 1)]
 
     send(st.at[1 - c], stp, sr_send, sr_recv, partner)
+    heard(1)
+    pass_on(2)
     arrived(stp, sr_recv)
     msg[0:6, :] = st[c, 0:6, :] + stp[0:6, :]
     msg[6:8, :] = jnp.zeros((2, 128), F32)
     msg[6:7, 0:40] = (snt[...] + sns[...]).reshape(1, 40)
     gath[z] = msg[...]
-    for d in range(1, nz):
+
+    def send_sums(d):
         send(msg, gath.at[z], g_send.at[d - 1], g_recv.at[d - 1], at(z + d, c))
+
+    for d in (2, nz - 2, 1, nz - 1):
+        send_sums(d)
+    send_raw(2)
+    heard(2)
+    pass_on(3)
+    for d in (3, nz - 3):
+        send_sums(d)
+    send_raw(3)
+    heard(3)
+    send_sums(4)
+    send_raw(4)
+
     for d in range(2):
+        mine = rlow.at[d, :, quarter(y)]
+        arrived(mine, low_recv.at[d])
+        for k in range(1, ny):
+            send(mine, mine, ly_send.at[d, k - 1], ly_recv.at[d, k - 1], rank_of(k))
+    for d in range(2):
+        for k in range(1, ny):
+            arrived(rlow.at[d, :, quarter(lax.rem(y - k + ny, ny))], ly_recv.at[d, k - 1])
         for a in range(3):
-            send(low[a], rl[a].at[d], low_send.at[d, a], low_recv.at[d, a], nbr[d])
-    for i in range(1, len(CHUNKS)):
-        send_raw(i)
+            product(rlow.at[d, a], high[a], prod.at[d], a)
 
     for d in range(1, nz):
         arrived(gath.at[lax.rem(z - d + nz, nz)], g_recv.at[d - 1])
@@ -124,9 +166,9 @@
     for k in range(1, nz):
         total = total + gath[k]
     fin[c] = total * (1.0 / d_model)
+    send(fin.at[c], fin.at[c], f_send, f_recv, partner)
     for k in range(nz):
         nrm[c, k : k + 1, :] = gath[k, 6:7, :]
-    send(fin.at[c], fin.at[c], f_send, f_recv, partner)
     send(nrm.at[c], nrm.at[c], n_send, n_recv, partner)
     arrived(fin.at[1 - c], f_recv)
     for j in range(12):
@@ -147,17 +189,6 @@
         return z - h * step[d]
 
     for i, (a, r0, n) in enumerate(CHUNKS):
-        dst = place(a, z, c, r0, n)
-        for t in range(0, COLS[a + 1] - COLS[a], TILE):
-            col = COLS[a] + t
-            dst[:, t : t + TILE] = (prod[2, r0 : r0 + n, col : col + TILE] * inv[:, col : col + TILE]).astype(BF16)
-        send(dst, dst, p_send.at[0, 0, i], p_recv.at[0, 0, i], partner)
-
-    for d in range(2):
-        for a in range(3):
-            arrived(rl[a].at[d], low_recv.at[d, a])
-            product(rl[a].at[d], high[a], prod.at[d], a)
-    for i, (a, r0, n) in enumerate(CHUNKS):
         for d in range(2):
             arrived(rw[a].at[d, pl.ds(r0, n)], r_recv.at[d, 0, i])
             dst = place(a, origin(d, 1), c, r0, n)
@@ -167,11 +198,17 @@
                 dst[:, t : t + TILE] = (fresh * inv[:, col : col + TILE]).astype(BF16)
             send(dst, dst, r_send.at[d, 1, i], r_recv.at[d, 1, i], nbr[d])
             send(dst, dst, p_send.at[d, 1, i], p_recv.at[d, 1, i], partner)
+    for i, (a, r0, n) in enumerate(CHUNKS):
+        dst = place(a, z, c, r0, n)
+        for t in range(0, COLS[a + 1] - COLS[a], TILE):
+            col = COLS[a] + t
+            dst[:, t : t + TILE] = (prod[2, r0 : r0 + n, col : col + TILE] * inv[:, col : col + TILE]).astype(BF16)
+        send(dst, dst, p_send.at[0, 0, i], p_recv.at[0, 0, i], partner)
 
     arrived(nrm.at[1 - c], n_recv)
     nall[y] = nrm[...]
-    for d in range(1, 4):
-        send(nrm, nall.at[y], y_send.at[d - 1], y_recv.at[d - 1], {"tp": lax.rem(y + d, 4)})
+    for d in range(1, ny):
+        send(nrm, nall.at[y], y_send.at[d - 1], y_recv.at[d - 1], rank_of(d))
 
     for h in (2, 3, 4):
         for i, (a, r0, n) in enumerate(CHUNKS):
@@ -184,10 +221,10 @@
                     send(dst, dst, r_send.at[d, h, i], r_recv.at[d, h, i], nbr[d])
                 send(dst, dst, p_send.at[d, h, i], p_recv.at[d, h, i], partner)
         if h == 2:
-            for d in range(1, 4):
-                arrived(nall.at[lax.rem(y - d + 4, 4)], y_recv.at[d - 1])
+            for d in range(1, ny):
+                arrived(nall.at[lax.rem(y - d + ny, ny)], y_recv.at[d - 1])
             for b in range(4):
-                for yy in range(4):
+                for yy in range(ny):
                     k = 4 * b + yy
                     for g in range(4):
                         s = 4 * g + b
@@ -211,7 +248,10 @@
 
 def flush(*refs):
     sem = refs[-1]
-    copies = [pltpu.make_async_copy(refs[i], refs[7 + i], sem.at[i]) for i in range(7)]
+    pairs = [(refs[i], refs[7 + i]) for i in range(1, 7)]
+    n = refs[0].shape[0] // 4
+    pairs = [(refs[0].at[pl.ds(k * n, n)], refs[7].at[pl.ds(k * n, n)]) for k in range(4)] + pairs
+    copies = [pltpu.make_async_copy(src, dst, sem.at[i]) for i, (src, dst) in enumerate(pairs)]
     for cp in copies:
         cp.start()
     for cp in copies:
@@ -234,12 +274,12 @@
     )
     scratch = (
         *(pltpu.VMEM((rows, m), BF16) for m in widths),
-        *(pltpu.VMEM((rank, rows), BF16) for _ in widths),
+        pltpu.VMEM((3, rank, rows), BF16),
         *(pltpu.VMEM((rank, m), BF16) for m in widths),
         pltpu.VMEM((40,), F32),
         pltpu.VMEM((40,), F32),
         *(pltpu.VMEM((2, rows, m), BF16) for m in widths),
-        *(pltpu.VMEM((2, rank, rows), BF16) for _ in widths),
+        pltpu.VMEM((2, 3, rank, rows), BF16),
         pltpu.VMEM((3, rows, wide), F32),
         pltpu.VMEM((2, 8, 128), F32),
         pltpu.VMEM((8, 128), F32),
@@ -252,10 +292,12 @@
         pltpu.VMEM((4, 640), F32),
         pltpu.VMEM((20, 128), F32),
         dma((11,)),
-        dma, dma, dma, dma,
+        pltpu.SemaphoreType.REGULAR((2, 3)),
+        dma, dma,
         dma((7,)), dma((7,)),
         dma, dma, dma, dma,
         dma((3,)), dma((3,)),
+        dma((2,)), dma((2,)),
         dma((2, 3)), dma((2, 3)),
         dma((2, 4, n)), dma((2, 4, n)),
         dma((2, 5, n)), dma((2, 5, n)),
@@ -276,7 +318,7 @@
         out_shape=tuple(jax.ShapeDtypeStruct(a.shape, a.dtype) for a in made),
         in_specs=[vm] * 7,
         out_specs=(pl.BlockSpec(memory_space=pltpu.HBM),) * 7,
-        scratch_shapes=(dma((7,)),),
+        scratch_shapes=(dma((10,)),),
         compiler_params=pltpu.CompilerParams(vmem_limit_bytes=1024 * 1024),
     )(*(pltpu.with_memory_space_constraint(a, pltpu.VMEM) for a in made))
     return oq, ok, ov, fq.reshape(-1), fk.reshape(-1), fv.reshape(-1), on.reshape(-1)

time: 58.5 us -> 59 us (level)
  no operation moved by 1% of the time
where the time goes in v2:
time: 59 us; the launch traced here: 58.9 us
  Pallas kernels  58.2 us (99%)
  between operations  0.64 us (1%)
    pallas_call x1, Pallas kernels, per_device(): pl.pallas_call(kernel, out_shape=out_shape, in_specs=[any_spec] * 11, out...  55 us
    pallas_call x1, Pallas kernels, per_device(): pl.pallas_call(flush, out_shape=tuple((jax.ShapeDtypeStruct(a.shape, a.dt...  3.28 us

profile of v2, /device:TPU:1, one launch (start us, length us, event | category | flops | bytes accessed | tf_op | source)
XLA Modules:
  0.0 58.9 jit_solution(7237595788529609908)
XLA Ops:
  0.6 55.0 %shard_map.162 = (bf16[2560,1024]{1,0:T(8,128)(2,1)S(1)}, bf16[2560,256]{1,0:T(8,128)(2,1)S(1)}, bf16[2560,256]{1,0:T(8,128)(2,1)S(1)}, f32[1,1024]{1,0:T(1,128)...) custom-call(bf16[160,1024]{1,0:T(8,128)(2,1)} %wq.1, bf16[64,160]{1,0:T(8,128)(2,1)} %bitcast.7, ...), custom_call_target="tpu_custom_call" | custom-call | tf_op jit(solution)/shard_map/pallas_call | solution.py:305
  55.6 3.3 %shard_map.163 = (bf16[2560,1024]{1,0:T(8,128)(2,1)}, bf16[2560,256]{1,0:T(8,128)(2,1)}, bf16[2560,256]{1,0:T(8,128)(2,1)}, f32[1,1024]{1,0:T(1,128)}, f32[1,256...) custom-call(bf16[2560,1024]{1,0:T(8,128)(2,1)S(1)} %get-tuple-element.21.refs_0_, ...), custom_call_target="tpu_custom_call" | custom-call | tf_op jit(solution)/shard_map/pallas_call | solution.py:316

commit v3 on v2

v3 whole, which is shorter than its diff:
```python
import functools

import jax
import jax.numpy as jnp
from jax import lax
from jax.experimental import pallas as pl
from jax.experimental.pallas import tpu as pltpu
from jax.sharding import PartitionSpec as P

MESH = pl.DeviceIdType.MESH
F32 = jnp.float32
BF16 = jnp.bfloat16

mix_rate = 1.0

RAW = ((0, 48), (48, 32), (80, 80))
EARLY = 1
HOP = ((0, 80), (80, 80))
LAST = ((0,), (1,))
TILE = 256
HALF = 6


def kernel(
    wq, lq, hq, wk, lk, hk, wv, lv, hv, nt, ns,
    out, fq, fk, fv, on,
    own, low, high, snt, sns, raw, rlow, prod, st, stp, msg, gath, fin, nall, inv, nout, nrow,
    load_sem, near, far, ranks, st_send, st_recv, g_send, g_recv, f_send, f_recv, y_send, y_recv, on_send, on_recv,
    low_send, low_recv, ly_send, ly_recv, raw_send, raw_recv, r_send, r_recv, p_send, p_recv,
):
    shard = lax.axis_index("shard")
    y = lax.axis_index("tp")
    z, c = shard // 2, shard % 2
    nz, ny = 8, 4
    rows, wide = own.shape
    d_model = rows * 16
    step = (1 - 2 * c, 2 * c - 1)

    def at(zz, cc):
        return {"shard": lax.rem(zz + 4 * nz, nz) * 2 + cc}

    def rank_of(d):
        return {"tp": lax.rem(y + d, ny)}

    partner = at(z, 1 - c)
    nbr = (at(z + step[0], c), at(z + step[1], c))

    nq, nk = wq.shape[1], wk.shape[1]
    parts = (pl.ds(0, nq), pl.ds(nq, nk), pl.ds(nq + nk, nk))
    pairs = (
        (lq, low.at[0]), (lk, low.at[1]), (lv, low.at[2]),
        (wq, own.at[:, parts[0]]), (wk, own.at[:, parts[1]]), (wv, own.at[:, parts[2]]),
        (hq, high.at[:, parts[0]]), (hk, high.at[:, parts[1]]), (hv, high.at[:, parts[2]]),
        (nt, snt), (ns, sns),
    )
    loads = [pltpu.make_async_copy(src, dst, load_sem.at[i]) for i, (src, dst) in enumerate(pairs)]
    for cp in loads:
        cp.start()

    barrier = pltpu.get_barrier_semaphore()

    def signal(sem, to):
        pl.semaphore_signal(sem, inc=1, device_id=to, device_id_type=MESH)

    for peer in (at(z - 1, 0), at(z + 1, 0)):
        signal(barrier, peer)

    @pl.when(c == 1)
    def _():
        signal(barrier, partner)

    @pl.when(c == 0)
    def _():
        pl.semaphore_wait(barrier, 5)
        signal(near, partner)

    @pl.when(c == 1)
    def _():
        pl.semaphore_wait(near, 1)
        for d in range(1, ny):
            signal(barrier, rank_of(d))

    def pass_on(k):
        for d in range(2):
            signal(far.at[d, k - 1], nbr[d])

    def heard(k):
        for d in range(2):
            pl.semaphore_wait(far.at[d, k - 1], 1)

    pass_on(1)

    sends = []

    def send(src, dst, s_sem, r_sem, to):
        cp = pltpu.make_async_remote_copy(
            src_ref=src, dst_ref=dst, send_sem=s_sem, recv_sem=r_sem, device_id=to, device_id_type=MESH
        )
        cp.start()
        sends.append(cp)

    def arrived(dst, sem):
        pltpu.make_async_remote_copy(
            src_ref=dst, dst_ref=dst, send_sem=sem, recv_sem=sem, device_id=partner, device_id_type=MESH
        ).wait_recv()

    def send_raw(i):
        piece = pl.ds(*RAW[i])
        for d in range(2):
            send(own.at[piece], raw.at[d, piece], raw_send.at[d, i], raw_recv.at[d, i], nbr[d])

    def quarter(rank):
        share = low.shape[1] // ny
        return pl.ds(pl.multiple_of(rank * share, share), share)

    for i in range(3):
        loads[i].wait()
    for d in range(2):
        send(low.at[:, quarter(y)], rlow.at[d, :, quarter(y)], low_send.at[d], low_recv.at[d], nbr[d])
    for i in range(3, 6):
        loads[i].wait()
    for i in range(EARLY):
        send_raw(i)
    for i in range(6, 11):
        loads[i].wait()

    def array_of(col):
        return 0 if col < nq else 1 if col < nq + nk else 2

    def product(l_ref, col):
        return mix_rate * lax.dot_general(
            l_ref[array_of(col)], high[:, col : col + TILE], (((0,), (0,)), ((), ())), preferred_element_type=F32
        )

    for col in range(0, wide, TILE):
        fresh = own[:, col : col + TILE].astype(F32) + product(low, col)
        prod[2, :, col : col + TILE] = fresh
        total = jnp.sum(jnp.abs(fresh), axis=0, keepdims=True)
        for g in range(TILE // 128):
            j = col // 128 + g
            st[j // HALF, j % HALF] = total[:, 128 * g : 128 * (g + 1)]
    send(st.at[1 - c], stp, st_send, st_recv, partner)
    heard(1)
    pass_on(2)
    msg[HALF] = jnp.zeros((1, 128), F32)
    msg[HALF, 0:1, 0:40] = (snt[...] + sns[...]).reshape(1, 40)
    arrived(stp, st_recv)
    msg[0:HALF] = st[c] + stp[...]
    gath[z] = msg[...]

    def send_sums(d):
        send(msg, gath.at[z], g_send.at[d - 1], g_recv.at[d - 1], at(z + d, c))

    for d in (2, nz - 2, 1, nz - 1):
        send_sums(d)
    heard(2)
    pass_on(3)
    for d in (3, nz - 3):
        send_sums(d)
    heard(3)
    send_sums(4)
    for i in range(EARLY, len(RAW)):
        send_raw(i)

    @pl.when(c == 1)
    def _():
        pl.semaphore_wait(barrier, ny - 1)
        signal(ranks, partner)

    @pl.when(c == 0)
    def _():
        pl.semaphore_wait(ranks, 1)

    for d in range(2):
        mine = rlow.at[d, :, quarter(y)]
        arrived(mine, low_recv.at[d])
        for k in range(1, ny):
            send(mine, mine, ly_send.at[d, k - 1], ly_recv.at[d, k - 1], rank_of(k))
    for d in range(2):
        for k in range(1, ny):
            arrived(rlow.at[d, :, quarter(lax.rem(y - k + ny, ny))], ly_recv.at[d, k - 1])
        for col in range(0, wide, TILE):
            prod[d, :, col : col + TILE] = product(rlow.at[d], col)

    for d in range(1, nz):
        arrived(gath.at[lax.rem(z - d + nz, nz)], g_recv.at[d - 1])
    total = gath[0, 0:HALF]
    for k in range(1, nz):
        total = total + gath[k, 0:HALF]
    fin[c, 0:HALF] = total * (1.0 / d_model)
    for k in range(nz):
        fin[c, HALF + k] = gath[k, HALF]
    send(fin.at[c], fin.at[c], f_send, f_recv, partner)
    arrived(fin.at[1 - c], f_recv)
    for j in range(2 * HALF):
        factor = fin[j // HALF, j % HALF]
        inv[:, 128 * j : 128 * (j + 1)] = 1.0 / factor
        if j < 8:
            fq[:, 128 * j : 128 * (j + 1)] = factor
        elif j < 10:
            fk[:, 128 * (j - 8) : 128 * (j - 7)] = factor
        else:
            fv[:, 128 * (j - 10) : 128 * (j - 9)] = factor

    def place(zz, cc, piece):
        first = pl.multiple_of((lax.rem(zz + 4 * nz, nz) * 2 + cc) * rows, 16)
        return out.at[pl.ds(first + piece[0], piece[1])]

    def origin(d, h):
        return z - h * step[d]

    def to_partner(d, h, i):
        dst = place(origin(d, h), c, HOP[i])
        send(dst, dst, p_send.at[d, h, i], p_recv.at[d, h, i], partner)

    def onward(d, h, i):
        dst = place(origin(d, h), c, HOP[i])
        send(dst, dst, r_send.at[d, h, i], r_recv.at[d, h, i], nbr[d])

    for i, (h0, hn) in enumerate(HOP):
        for d in range(2):
            for j, (r0, n) in enumerate(RAW):
                if not h0 <= r0 < h0 + hn:
                    continue
                arrived(raw.at[d, pl.ds(r0, n)], raw_recv.at[d, j])
                dst = place(origin(d, 1), c, (r0, n))
                for col in range(0, wide, TILE):
                    fresh = raw[d, r0 : r0 + n, col : col + TILE].astype(F32) + prod[d, r0 : r0 + n, col : col + TILE]
                    dst[:, col : col + TILE] = (fresh * inv[:, col : col + TILE]).astype(BF16)
            onward(d, 1, i)
            to_partner(d, 1, i)
    dst = place(z, c, (0, rows))
    for col in range(0, wide, TILE):
        dst[:, col : col + TILE] = (prod[2, :, col : col + TILE] * inv[:, col : col + TILE]).astype(BF16)
    send(dst, dst, p_send.at[0, 0, 0], p_recv.at[0, 0, 0], partner)

    gains = fin.at[:, pl.ds(HALF, nz)]
    to_ranks = [
        pltpu.make_async_remote_copy(
            src_ref=gains, dst_ref=nall.at[y], send_sem=y_send.at[d - 1], recv_sem=y_recv.at[d - 1],
            device_id=rank_of(d), device_id_type=MESH,
        )
        for d in range(1, ny)
    ]
    to_core0 = pltpu.make_async_remote_copy(
        src_ref=on, dst_ref=on, send_sem=on_send, recv_sem=on_recv, device_id=partner, device_id_type=MESH
    )

    @pl.when(c == 1)
    def _():
        for cp in to_ranks:
            cp.start()
        nall[y] = fin[:, HALF : HALF + nz]

    for h in (2, 3, 4):
        for i in range(len(HOP)):
            for d in range(2):
                if h == 4 and i not in LAST[d]:
                    continue
                arrived(place(origin(d, h), c, HOP[i]), r_recv.at[d, h - 1, i])
                if h == 2 or (h == 3 and i in LAST[d]):
                    onward(d, h, i)
                to_partner(d, h, i)
        if h == 2:

            @pl.when(c == 1)
            def _():
                for d in range(1, ny):
                    arrived(nall.at[lax.rem(y - d + ny, ny)], y_recv.at[d - 1])
                for b in range(4):
                    for yy in range(ny):
                        k = 4 * b + yy
                        for g in range(4):
                            s = 4 * g + b
                            nout[g : g + 1, 40 * k : 40 * k + 40] = nall[yy, s % 2, s // 2, :, 0:40]
                for g in range(4):
                    for j in range(5):
                        nrow[5 * g + j : 5 * g + j + 1, :] = nout[g : g + 1, 128 * j : 128 * (j + 1)]
                on[...] = nrow[...].astype(BF16)
                to_core0.start()

    arrived(place(z, 1 - c, (0, rows)), p_recv.at[0, 0, 0])
    for h in (1, 2, 3, 4):
        for i in range(len(HOP)):
            for d in range(2):
                if h == 4 and i not in LAST[d]:
                    continue
                arrived(place(z + h * step[d], 1 - c, HOP[i]), p_recv.at[d, h, i])
    for cp in sends:
        cp.wait_send()

    @pl.when(c == 1)
    def _():
        for cp in (*to_ranks, to_core0):
            cp.wait_send()

    @pl.when(c == 0)
    def _():
        to_core0.wait_recv()


def flush(out, fq, fk, fv, on, oq, ok, ov, gq, gk, gv, gn, sem):
    nq, nk = oq.shape[1], ok.shape[1]
    n = out.shape[0] // 4
    pairs = [(fq, gq), (fk, gk), (fv, gv), (on, gn)]
    for k in range(4):
        piece = pl.ds(k * n, n)
        for dst, first, m in ((oq, 0, nq), (ok, nq, nk), (ov, nq + nk, nk)):
            pairs.append((out.at[piece, pl.ds(first, m)], dst.at[piece]))
    copies = [pltpu.make_async_copy(src, dst, sem.at[i]) for i, (src, dst) in enumerate(pairs)]
    for cp in copies:
        cp.start()
    for cp in copies:
        cp.wait()


def per_device(wq, lq, hq, wk, lk, hk, wv, lv, hv, nt, ns):
    rows = wq.shape[0]
    dma = pltpu.SemaphoreType.DMA
    hbm = pl.BlockSpec(memory_space=pltpu.HBM)
    vm = pl.BlockSpec(memory_space=pltpu.VMEM)
    widths = (wq.shape[1], wk.shape[1], wv.shape[1])
    rank = hq.shape[0]
    wide = sum(widths)
    out_shape = (
        pltpu.VMEM((16 * rows, wide), BF16),
        *(pltpu.VMEM((1, m), F32) for m in widths),
        pltpu.VMEM((20, 128), BF16),
    )
    scratch = (
        pltpu.VMEM((rows, wide), BF16),
        pltpu.VMEM((3, rank, rows), BF16),
        pltpu.VMEM((rank, wide), BF16),
        pltpu.VMEM((40,), F32),
        pltpu.VMEM((40,), F32),
        pltpu.VMEM((2, rows, wide), BF16),
        pltpu.VMEM((2, 3, rank, rows), BF16),
        pltpu.VMEM((3, rows, wide), F32),
        pltpu.VMEM((2, HALF, 1, 128), F32),
        pltpu.VMEM((HALF, 1, 128), F32),
        pltpu.VMEM((HALF + 1, 1, 128), F32),
        pltpu.VMEM((8, HALF + 1, 1, 128), F32),
        pltpu.VMEM((2, HALF + 8, 1, 128), F32),
        pltpu.VMEM((4, 2, 8, 1, 128), F32),
        pltpu.VMEM((1, wide), F32),
        pltpu.VMEM((4, 640), F32),
        pltpu.VMEM((20, 128), F32),
        dma((11,)),
        pltpu.SemaphoreType.REGULAR,
        pltpu.SemaphoreType.REGULAR((2, 3)),
        pltpu.SemaphoreType.REGULAR,
        dma, dma,
        dma((7,)), dma((7,)),
        dma, dma,
        dma((3,)), dma((3,)),
        dma, dma,
        dma((2,)), dma((2,)),
        dma((2, 3)), dma((2, 3)),
        dma((2, len(RAW))), dma((2, len(RAW))),
        dma((2, 4, len(HOP))), dma((2, 4, len(HOP))),
        dma((2, 5, len(HOP))), dma((2, 5, len(HOP))),
    )
    made = pl.pallas_call(
        kernel,
        out_shape=out_shape,
        in_specs=[hbm] * 11,
        out_specs=(vm,) * 5,
        scratch_shapes=scratch,
        compiler_params=pltpu.CompilerParams(
            collective_id=0, has_side_effects=True, vmem_limit_bytes=24 * 1024 * 1024
        ),
    )(*(pltpu.with_memory_space_constraint(a, pltpu.HBM) for a in (wq, lq.T, hq, wk, lk.T, hk, wv, lv.T, hv, nt, ns)))
    oq, ok, ov, fq, fk, fv, on = pl.pallas_call(
        flush,
        out_shape=(
            *(jax.ShapeDtypeStruct((16 * rows, m), BF16) for m in widths),
            *(jax.ShapeDtypeStruct((1, m), F32) for m in widths),
            jax.ShapeDtypeStruct((20, 128), BF16),
        ),
        in_specs=[vm] * 5,
        out_specs=(hbm,) * 7,
        scratch_shapes=(dma((16,)),),
        compiler_params=pltpu.CompilerParams(vmem_limit_bytes=1024 * 1024),
    )(*(pltpu.with_memory_space_constraint(a, pltpu.VMEM) for a in made))
    return oq, ok, ov, fq.reshape(-1), fk.reshape(-1), fv.reshape(-1), on.reshape(-1)


def solution(mesh):
    return jax.shard_map(
        per_device,
        mesh=mesh,
        in_specs=(
            P(("shift", "shard"), "tp"),
            P(("shift", "shard"), None),
            P("shift", "tp"),
            P(("shift", "shard"), "tp"),
            P(("shift", "shard"), None),
            P("shift", "tp"),
            P(("shift", "shard"), "tp"),
            P(("shift", "shard"), None),
            P("shift", "tp"),
            P(("shift", "shard", "tp")),
            P(("shift", "shard", "tp")),
        ),
        out_specs=(
            P("shift", "tp"),
            P("shift", "tp"),
            P("shift", "tp"),
            P(("shift", "tp")),
            P(("shift", "tp")),
            P(("shift", "tp")),
            P("shift"),
        ),
        check_vma=False,
    )
```

time: 59 us -> 54.3 us (0.920)
  Pallas kernels: 58.2 us -> 53.5 us
    pallas_call x2, Pallas kernels: 58.2 us -> 53.5 us  [the longest x1 50.2 us: per_device(): pl.pallas_call(kernel, out_shape=out_shape, in_specs=[hbm] * 11, out_spec...]
where the time goes in v3:
time: 54.3 us; the launch traced here: 54.2 us
  Pallas kernels  53.5 us (99%)
  between operations  0.64 us (1%)
    pallas_call x1, Pallas kernels, per_device(): pl.pallas_call(kernel, out_shape=out_shape, in_specs=[hbm] * 11, out_spec...  50.2 us
    pallas_call x1, Pallas kernels, per_device(): pl.pallas_call(flush, out_shape=(*(jax.ShapeDtypeStruct((16 * rows, m), B...  3.3 us

profile of v3, /device:TPU:1, one launch (start us, length us, event | category | flops | bytes accessed | tf_op | source)
XLA Modules:
  0.0 54.2 jit_solution(4845749275981991835)
XLA Ops:
  0.6 50.2 %shard_map.162 = (bf16[2560,1536]{1,0:T(8,128)(2,1)S(1)}, f32[1,1024]{1,0:T(1,128)S(1)}, f32[1,256]{1,0:T(1,128)S(1)}, f32[1,256]{1,0:T(1,128)S(1)}, bf16[20,128]{1,0:T(8,128)(2,1)S(1)}) custom-call(bf16[160,1024]{1,0:T(8,128)(2,1)} %wq.1, bf16[64,160]{1,0:T(8,128)(2,1)} %bitcast.7, bf16[64,1024]{1,0:T(8,128)(2,1)} %hq.1, bf16[160,256]{1,0:T(8,128)(2,1)} %wk.1, ...), custom_call_target="tpu_custom_call" | custom-call | tf_op jit(solution)/shard_map/pallas_call | solution.py:363
  50.9 3.3 %shard_map.163 = (bf16[2560,1024]{1,0:T(8,128)(2,1)}, bf16[2560,256]{1,0:T(8,128)(2,1)}, bf16[2560,256]{1,0:T(8,128)(2,1)}, f32[1,1024]{1,0:T(1,128)}, f32[1,256...) custom-call(bf16[2560,1536]{1,0:T(8,128)(2,1)S(1)} %get-tuple-element.19.out, ...), custom_call_target="tpu_custom_call" | custom-call | tf_op jit(solution)/shard_map/pallas_call | solution.py:373

commit v4 on v3

--- a/solution.py
+++ b/solution.py
@@ -13,18 +13,17 @@
 
 mix_rate = 1.0
 
-RAW = ((0, 48), (48, 32), (80, 80))
-EARLY = 1
+RAW = (((0, 80), (80, 80)),) * 2
 HOP = ((0, 80), (80, 80))
 LAST = ((0,), (1,))
 TILE = 256
-HALF = 6
+GROUPS = 12
 
 
 def kernel(
     wq, lq, hq, wk, lk, hk, wv, lv, hv, nt, ns,
     out, fq, fk, fv, on,
-    own, low, high, snt, sns, raw, rlow, prod, st, stp, msg, gath, fin, nall, inv, nout, nrow,
+    own, low, high, snt, sns, raw, rlow, prod, st, stp, sums, gains, nall, inv, nout, nrow,
     load_sem, near, far, ranks, st_send, st_recv, g_send, g_recv, f_send, f_recv, y_send, y_recv, on_send, on_recv,
     low_send, low_recv, ly_send, ly_recv, raw_send, raw_recv, r_send, r_recv, p_send, p_recv,
 ):
@@ -62,31 +61,29 @@
     def signal(sem, to):
         pl.semaphore_signal(sem, inc=1, device_id=to, device_id_type=MESH)
 
-    for peer in (at(z - 1, 0), at(z + 1, 0)):
+    for peer in (at(z - 1, 1), at(z + 1, 1)):
         signal(barrier, peer)
 
+    @pl.when(c == 0)
+    def _():
+        signal(barrier, partner)
+
     @pl.when(c == 1)
-    def _():
-        signal(barrier, partner)
-
-    @pl.when(c == 0)
     def _():
         pl.semaphore_wait(barrier, 5)
         signal(near, partner)
 
-    @pl.when(c == 1)
+    @pl.when(c == 0)
     def _():
         pl.semaphore_wait(near, 1)
         for d in range(1, ny):
             signal(barrier, rank_of(d))
 
     def pass_on(k):
-        for d in range(2):
-            signal(far.at[d, k - 1], nbr[d])
+        signal(far.at[k - 1], nbr[0])
 
     def heard(k):
-        for d in range(2):
-            pl.semaphore_wait(far.at[d, k - 1], 1)
+        pl.semaphore_wait(far.at[k - 1], 1)
 
     pass_on(1)
 
@@ -104,10 +101,9 @@
             src_ref=dst, dst_ref=dst, send_sem=sem, recv_sem=sem, device_id=partner, device_id_type=MESH
         ).wait_recv()
 
-    def send_raw(i):
-        piece = pl.ds(*RAW[i])
-        for d in range(2):
-            send(own.at[piece], raw.at[d, piece], raw_send.at[d, i], raw_recv.at[d, i], nbr[d])
+    def send_raw(d, i):
+        piece = pl.ds(*RAW[d][i])
+        send(own.at[piece], raw.at[d, piece], raw_send.at[d, i], raw_recv.at[d, i], nbr[d])
 
     def quarter(rank):
         share = low.shape[1] // ny
@@ -119,8 +115,8 @@
         send(low.at[:, quarter(y)], rlow.at[d, :, quarter(y)], low_send.at[d], low_recv.at[d], nbr[d])
     for i in range(3, 6):
         loads[i].wait()
-    for i in range(EARLY):
-        send_raw(i)
+    for d in range(2):
+        send_raw(d, 0)
     for i in range(6, 11):
         loads[i].wait()
 
@@ -138,36 +134,47 @@
         total = jnp.sum(jnp.abs(fresh), axis=0, keepdims=True)
         for g in range(TILE // 128):
             j = col // 128 + g
-            st[j // HALF, j % HALF] = total[:, 128 * g : 128 * (g + 1)]
-    send(st.at[1 - c], stp, st_send, st_recv, partner)
+            st[j] = total[:, 128 * g : 128 * (g + 1)]
+    st[GROUPS] = jnp.zeros((1, 128), F32)
+    st[GROUPS, 0:1, 0:40] = (snt[...] + sns[...]).reshape(1, 40)
+    send(st, stp, st_send, st_recv, partner)
     heard(1)
     pass_on(2)
-    msg[HALF] = jnp.zeros((1, 128), F32)
-    msg[HALF, 0:1, 0:40] = (snt[...] + sns[...]).reshape(1, 40)
     arrived(stp, st_recv)
-    msg[0:HALF] = st[c] + stp[...]
-    gath[z] = msg[...]
-
-    def send_sums(d):
-        send(msg, gath.at[z], g_send.at[d - 1], g_recv.at[d - 1], at(z + d, c))
-
-    for d in (2, nz - 2, 1, nz - 1):
-        send_sums(d)
+    sums[0, 0:GROUPS] = st[0:GROUPS] + stp[0:GROUPS]
+    sums[0, GROUPS + c] = st[GROUPS]
+    sums[0, GROUPS + 1 - c] = stp[GROUPS]
+
+    def slot(k):
+        return k + c * (nz - 2 * k)
+
+    def chips_sums(k):
+        return pltpu.make_async_remote_copy(
+            src_ref=sums.at[0], dst_ref=sums.at[slot(k)], send_sem=g_send.at[k - 1], recv_sem=g_recv.at[k - 1],
+            device_id=at(z + k * step[1], c), device_id_type=MESH,
+        )
+
+    for k in (1, 2):
+        chips_sums(k).start()
     heard(2)
     pass_on(3)
-    for d in (3, nz - 3):
-        send_sums(d)
+    chips_sums(3).start()
     heard(3)
-    send_sums(4)
-    for i in range(EARLY, len(RAW)):
-        send_raw(i)
 
     @pl.when(c == 1)
+    def _():
+        chips_sums(4).start()
+
+    for i in range(1, len(RAW[1])):
+        for d in range(2):
+            send_raw(d, i)
+
+    @pl.when(c == 0)
     def _():
         pl.semaphore_wait(barrier, ny - 1)
         signal(ranks, partner)
 
-    @pl.when(c == 0)
+    @pl.when(c == 1)
     def _():
         pl.semaphore_wait(ranks, 1)
 
@@ -182,18 +189,32 @@
         for col in range(0, wide, TILE):
             prod[d, :, col : col + TILE] = product(rlow.at[d], col)
 
-    for d in range(1, nz):
-        arrived(gath.at[lax.rem(z - d + nz, nz)], g_recv.at[d - 1])
-    total = gath[0, 0:HALF]
+    def swap(first, n):
+        part = sums.at[pl.ds(first, n)]
+        return pltpu.make_async_remote_copy(
+            src_ref=part, dst_ref=part, send_sem=f_send, recv_sem=f_recv, device_id=partner, device_id_type=MESH
+        )
+
+    for k in (1, 2, 3):
+        chips_sums(k).wait_recv()
+
+    @pl.when(c == 0)
+    def _():
+        swap(1, 3).start()
+        swap(4, 4).wait_recv()
+
+    @pl.when(c == 1)
+    def _():
+        chips_sums(4).wait_recv()
+        swap(4, 4).start()
+        swap(1, 3).wait_recv()
+
+    total = sums[lax.rem(nz - z, nz), 0:GROUPS]
     for k in range(1, nz):
-        total = total + gath[k, 0:HALF]
-    fin[c, 0:HALF] = total * (1.0 / d_model)
-    for k in range(nz):
-        fin[c, HALF + k] = gath[k, HALF]
-    send(fin.at[c], fin.at[c], f_send, f_recv, partner)
-    arrived(fin.at[1 - c], f_recv)
-    for j in range(2 * HALF):
-        factor = fin[j // HALF, j % HALF]
+        total = total + sums[lax.rem(k - z + nz, nz), 0:GROUPS]
+    total = total * (1.0 / d_model)
+    for j in range(GROUPS):
+        factor = total[j]
         inv[:, 128 * j : 128 * (j + 1)] = 1.0 / factor
         if j < 8:
             fq[:, 128 * j : 128 * (j + 1)] = factor
@@ -219,7 +240,7 @@
 
     for i, (h0, hn) in enumerate(HOP):
         for d in range(2):
-            for j, (r0, n) in enumerate(RAW):
+            for j, (r0, n) in enumerate(RAW[d]):
                 if not h0 <= r0 < h0 + hn:
                     continue
                 arrived(raw.at[d, pl.ds(r0, n)], raw_recv.at[d, j])
@@ -234,7 +255,6 @@
         dst[:, col : col + TILE] = (prod[2, :, col : col + TILE] * inv[:, col : col + TILE]).astype(BF16)
     send(dst, dst, p_send.at[0, 0, 0], p_recv.at[0, 0, 0], partner)
 
-    gains = fin.at[:, pl.ds(HALF, nz)]
     to_ranks = [
         pltpu.make_async_remote_copy(
             src_ref=gains, dst_ref=nall.at[y], send_sem=y_send.at[d - 1], recv_sem=y_recv.at[d - 1],
@@ -242,15 +262,17 @@
         )
         for d in range(1, ny)
     ]
-    to_core0 = pltpu.make_async_remote_copy(
+    to_partner_norm = pltpu.make_async_remote_copy(
         src_ref=on, dst_ref=on, send_sem=on_send, recv_sem=on_recv, device_id=partner, device_id_type=MESH
     )
 
-    @pl.when(c == 1)
-    def _():
+    @pl.when(c == 0)
+    def _():
+        for k in range(nz):
+            gains[k] = sums[lax.rem(k - z + nz, nz), GROUPS : GROUPS + 2]
+        nall[y] = gains[...]
         for cp in to_ranks:
             cp.start()
-        nall[y] = fin[:, HALF : HALF + nz]
 
     for h in (2, 3, 4):
         for i in range(len(HOP)):
@@ -263,7 +285,7 @@
                 to_partner(d, h, i)
         if h == 2:
 
-            @pl.when(c == 1)
+            @pl.when(c == 0)
             def _():
                 for d in range(1, ny):
                     arrived(nall.at[lax.rem(y - d + ny, ny)], y_recv.at[d - 1])
@@ -272,12 +294,12 @@
                         k = 4 * b + yy
                         for g in range(4):
                             s = 4 * g + b
-                            nout[g : g + 1, 40 * k : 40 * k + 40] = nall[yy, s % 2, s // 2, :, 0:40]
+                            nout[g : g + 1, 40 * k : 40 * k + 40] = nall[yy, s // 2, s % 2, :, 0:40]
                 for g in range(4):
                     for j in range(5):
                         nrow[5 * g + j : 5 * g + j + 1, :] = nout[g : g + 1, 128 * j : 128 * (j + 1)]
                 on[...] = nrow[...].astype(BF16)
-                to_core0.start()
+                to_partner_norm.start()
 
     arrived(place(z, 1 - c, (0, rows)), p_recv.at[0, 0, 0])
     for h in (1, 2, 3, 4):
@@ -289,14 +311,20 @@
     for cp in sends:
         cp.wait_send()
 
+    for k in (1, 2, 3):
+        chips_sums(k).wait_send()
+
     @pl.when(c == 1)
     def _():
-        for cp in (*to_ranks, to_core0):
+        for cp in (chips_sums(4), swap(4, 4)):
             cp.wait_send()
-
-    @pl.when(c == 0)
-    def _():
-        to_core0.wait_recv()
+        to_partner_norm.wait_recv()
+
+    @pl.when(c == 0)
+    def _():
+        swap(1, 3).wait_send()
+        for cp in (*to_ranks, to_partner_norm):
+            cp.wait_send()
 
 
 def flush(out, fq, fk, fv, on, oq, ok, ov, gq, gk, gv, gn, sem):
@@ -336,27 +364,26 @@
         pltpu.VMEM((2, rows, wide), BF16),
         pltpu.VMEM((2, 3, rank, rows), BF16),
         pltpu.VMEM((3, rows, wide), F32),
-        pltpu.VMEM((2, HALF, 1, 128), F32),
-        pltpu.VMEM((HALF, 1, 128), F32),
-        pltpu.VMEM((HALF + 1, 1, 128), F32),
-        pltpu.VMEM((8, HALF + 1, 1, 128), F32),
-        pltpu.VMEM((2, HALF + 8, 1, 128), F32),
-        pltpu.VMEM((4, 2, 8, 1, 128), F32),
+        pltpu.VMEM((GROUPS + 1, 1, 128), F32),
+        pltpu.VMEM((GROUPS + 1, 1, 128), F32),
+        pltpu.VMEM((8, GROUPS + 2, 1, 128), F32),
+        pltpu.VMEM((8, 2, 1, 128), F32),
+        pltpu.VMEM((4, 8, 2, 1, 128), F32),
         pltpu.VMEM((1, wide), F32),
         pltpu.VMEM((4, 640), F32),
         pltpu.VMEM((20, 128), F32),
         dma((11,)),
         pltpu.SemaphoreType.REGULAR,
-        pltpu.SemaphoreType.REGULAR((2, 3)),
+        pltpu.SemaphoreType.REGULAR((3,)),
         pltpu.SemaphoreType.REGULAR,
         dma, dma,
-        dma((7,)), dma((7,)),
+        dma((4,)), dma((4,)),
         dma, dma,
         dma((3,)), dma((3,)),
         dma, dma,
         dma((2,)), dma((2,)),
         dma((2, 3)), dma((2, 3)),
-        dma((2, len(RAW))), dma((2, len(RAW))),
+        dma((2, len(RAW[1]))), dma((2, len(RAW[1]))),
         dma((2, 4, len(HOP))), dma((2, 4, len(HOP))),
         dma((2, 5, len(HOP))), dma((2, 5, len(HOP))),
     )

time: 54.3 us -> 53.7 us (0.989)
  no operation moved by 1% of the time
where the time goes in v4:
time: 53.7 us; the launch traced here: 53.6 us
  Pallas kernels  53 us (99%)
  between operations  0.64 us (1%)
    pallas_call x1, Pallas kernels, per_device(): pl.pallas_call(kernel, out_shape=out_shape, in_specs=[hbm] * 11, out_spec...  49.7 us
    pallas_call x1, Pallas kernels, per_device(): pl.pallas_call(flush, out_shape=(*(jax.ShapeDtypeStruct((16 * rows, m), B...  3.3 us

profile of v4, /device:TPU:1, one launch (start us, length us, event | category | flops | bytes accessed | tf_op | source)
XLA Modules:
  0.0 53.6 jit_solution(2652806841269212144)
XLA Ops:
  0.6 49.7 %shard_map.162 = (bf16[2560,1536]{1,0:T(8,128)(2,1)S(1)}, f32[1,1024]{1,0:T(1,128)S(1)}, f32[1,256]{1,0:T(1,128)S(1)}, f32[1,256]{1,0:T(1,128)S(1)}, bf16[20,128]{1,0:T(8,128)(2,1)S(1)}) custom-call(bf16[160,1024]{1,0:T(8,128)(2,1)} %wq.1, bf16[64,160]{1,0:T(8,128)(2,1)} %bitcast.7, bf16[64,1024]{1,0:T(8,128)(2,1)} %hq.1, bf16[160,256]{1,0:T(8,128)(2,1)} %wk.1, ...), custom_call_target="tpu_custom_call" | custom-call | tf_op jit(solution)/shard_map/pallas_call | solution.py:390
  50.3 3.3 %shard_map.163 = (bf16[2560,1024]{1,0:T(8,128)(2,1)}, bf16[2560,256]{1,0:T(8,128)(2,1)}, bf16[2560,256]{1,0:T(8,128)(2,1)}, f32[1,1024]{1,0:T(1,128)}, f32[1,256...) custom-call(bf16[2560,1536]{1,0:T(8,128)(2,1)S(1)} %get-tuple-element.19.out, ...), custom_call_target="tpu_custom_call" | custom-call | tf_op jit(solution)/shard_map/pallas_call | solution.py:400

commit v5 on v4

--- a/solution.py
+++ b/solution.py
@@ -23,7 +23,7 @@
 def kernel(
     wq, lq, hq, wk, lk, hk, wv, lv, hv, nt, ns,
     out, fq, fk, fv, on,
-    own, low, high, snt, sns, raw, rlow, prod, st, stp, sums, gains, nall, inv, nout, nrow,
+    own, low, high, snt, sns, raw, pack, rlow, prod, st, stp, sums, gains, nall, inv, nout, nrow,
     load_sem, near, far, ranks, st_send, st_recv, g_send, g_recv, f_send, f_recv, y_send, y_recv, on_send, on_recv,
     low_send, low_recv, ly_send, ly_recv, raw_send, raw_recv, r_send, r_recv, p_send, p_recv,
 ):
@@ -111,10 +111,16 @@
 
     for i in range(3):
         loads[i].wait()
-    for d in range(2):
-        send(low.at[:, quarter(y)], rlow.at[d, :, quarter(y)], low_send.at[d], low_recv.at[d], nbr[d])
+    rest = rows - 128
+    pack[:, 384:512] = jnp.zeros((pack.shape[0], 128), BF16)
+    for a in range(3):
+        share = low[a, quarter(y), :]
+        pack[:, 128 * a : 128 * (a + 1)] = share[:, 0:128]
+        pack[:, 384 + rest * a : 384 + rest * (a + 1)] = share[:, 128:rows]
     for i in range(3, 6):
         loads[i].wait()
+    for d in range(2):
+        send(pack, rlow.at[d, quarter(y)], low_send.at[d], low_recv.at[d], nbr[d])
     for d in range(2):
         send_raw(d, 0)
     for i in range(6, 11):
@@ -123,13 +129,13 @@
     def array_of(col):
         return 0 if col < nq else 1 if col < nq + nk else 2
 
-    def product(l_ref, col):
+    def product(factor, col):
         return mix_rate * lax.dot_general(
-            l_ref[array_of(col)], high[:, col : col + TILE], (((0,), (0,)), ((), ())), preferred_element_type=F32
+            factor, high[:, col : col + TILE], (((0,), (0,)), ((), ())), preferred_element_type=F32
         )
 
     for col in range(0, wide, TILE):
-        fresh = own[:, col : col + TILE].astype(F32) + product(low, col)
+        fresh = own[:, col : col + TILE].astype(F32) + product(low[array_of(col)], col)
         prod[2, :, col : col + TILE] = fresh
         total = jnp.sum(jnp.abs(fresh), axis=0, keepdims=True)
         for g in range(TILE // 128):
@@ -179,15 +185,17 @@
         pl.semaphore_wait(ranks, 1)
 
     for d in range(2):
-        mine = rlow.at[d, :, quarter(y)]
+        mine = rlow.at[d, quarter(y)]
         arrived(mine, low_recv.at[d])
         for k in range(1, ny):
             send(mine, mine, ly_send.at[d, k - 1], ly_recv.at[d, k - 1], rank_of(k))
     for d in range(2):
         for k in range(1, ny):
-            arrived(rlow.at[d, :, quarter(lax.rem(y - k + ny, ny))], ly_recv.at[d, k - 1])
+            arrived(rlow.at[d, quarter(lax.rem(y - k + ny, ny))], ly_recv.at[d, k - 1])
         for col in range(0, wide, TILE):
-            prod[d, :, col : col + TILE] = product(rlow.at[d], col)
+            a = array_of(col)
+            prod[d, 0:128, col : col + TILE] = product(rlow[d, :, 128 * a : 128 * (a + 1)], col)
+            prod[d, 128:rows, col : col + TILE] = product(rlow[d, :, 384 + rest * a : 384 + rest * (a + 1)], col)
 
     def swap(first, n):
         part = sums.at[pl.ds(first, n)]
@@ -362,7 +370,8 @@
         pltpu.VMEM((40,), F32),
         pltpu.VMEM((40,), F32),
         pltpu.VMEM((2, rows, wide), BF16),
-        pltpu.VMEM((2, 3, rank, rows), BF16),
+        pltpu.VMEM((rank // 4, 512), BF16),
+        pltpu.VMEM((2, rank, 512), BF16),
         pltpu.VMEM((3, rows, wide), F32),
         pltpu.VMEM((GROUPS + 1, 1, 128), F32),
         pltpu.VMEM((GROUPS + 1, 1, 128), F32),

time: 53.7 us -> 53.6 us (level)
  no operation moved by 1% of the time
where the time goes in v5:
time: 53.6 us; the launch traced here: 53.5 us
  Pallas kernels  52.9 us (99%)
  between operations  0.64 us (1%)
    pallas_call x1, Pallas kernels, per_device(): pl.pallas_call(kernel, out_shape=out_shape, in_specs=[hbm] * 11, out_spec...  49.6 us
    pallas_call x1, Pallas kernels, per_device(): pl.pallas_call(flush, out_shape=(*(jax.ShapeDtypeStruct((16 * rows, m), B...  3.3 us

profile of v5, /device:TPU:1, one launch (start us, length us, event | category | flops | bytes accessed | tf_op | source)
XLA Modules:
  0.0 53.5 jit_solution(14665274245795747449)
XLA Ops:
  0.6 49.6 %shard_map.162 = (bf16[2560,1536]{1,0:T(8,128)(2,1)S(1)}, f32[1,1024]{1,0:T(1,128)S(1)}, f32[1,256]{1,0:T(1,128)S(1)}, f32[1,256]{1,0:T(1,128)S(1)}, bf16[20,128]{1,0:T(8,128)(2,1)S(1)}) custom-call(bf16[160,1024]{1,0:T(8,128)(2,1)} %wq.1, bf16[64,160]{1,0:T(8,128)(2,1)} %bitcast.7, bf16[64,1024]{1,0:T(8,128)(2,1)} %hq.1, bf16[160,256]{1,0:T(8,128)(2,1)} %wk.1, ...), custom_call_target="tpu_custom_call" | custom-call | tf_op jit(solution)/shard_map/pallas_call | solution.py:399
  50.2 3.3 %shard_map.163 = (bf16[2560,1024]{1,0:T(8,128)(2,1)}, bf16[2560,256]{1,0:T(8,128)(2,1)}, bf16[2560,256]{1,0:T(8,128)(2,1)}, f32[1,1024]{1,0:T(1,128)}, f32[1,256...) custom-call(bf16[2560,1536]{1,0:T(8,128)(2,1)S(1)} %get-tuple-element.19.out, ...), custom_call_target="tpu_custom_call" | custom-call | tf_op jit(solution)/shard_map/pallas_call | solution.py:409

commit v6 on v4

--- a/solution.py
+++ b/solution.py
@@ -248,8 +248,8 @@
                 for col in range(0, wide, TILE):
                     fresh = raw[d, r0 : r0 + n, col : col + TILE].astype(F32) + prod[d, r0 : r0 + n, col : col + TILE]
                     dst[:, col : col + TILE] = (fresh * inv[:, col : col + TILE]).astype(BF16)
+            to_partner(d, 1, i)
             onward(d, 1, i)
-            to_partner(d, 1, i)
     dst = place(z, c, (0, rows))
     for col in range(0, wide, TILE):
         dst[:, col : col + TILE] = (prod[2, :, col : col + TILE] * inv[:, col : col + TILE]).astype(BF16)
@@ -276,7 +276,7 @@
 
     for h in (2, 3, 4):
         for i in range(len(HOP)):
-            for d in range(2):
+            for d in (1, 0):
                 if h == 4 and i not in LAST[d]:
                     continue
                 arrived(place(origin(d, h), c, HOP[i]), r_recv.at[d, h - 1, i])

time: 53.7 us -> 53.5 us (level)
  no operation moved by 1% of the time
where the time goes in v6:
time: 53.5 us
  Pallas kernels  52.8 us (99%)
  between operations  0.64 us (1%)
    pallas_call x1, Pallas kernels, per_device(): pl.pallas_call(kernel, out_shape=out_shape, in_specs=[hbm] * 11, out_spec...  49.5 us
    pallas_call x1, Pallas kernels, per_device(): pl.pallas_call(flush, out_shape=(*(jax.ShapeDtypeStruct((16 * rows, m), B...  3.3 us

profile of v6, /device:TPU:1, one launch (start us, length us, event | category | flops | bytes accessed | tf_op | source)
XLA Modules:
  0.0 53.5 jit_solution(11097325999424873780)
XLA Ops:
  0.6 49.5 %shard_map.162 = (bf16[2560,1536]{1,0:T(8,128)(2,1)S(1)}, f32[1,1024]{1,0:T(1,128)S(1)}, f32[1,256]{1,0:T(1,128)S(1)}, f32[1,256]{1,0:T(1,128)S(1)}, bf16[20,128]{1,0:T(8,128)(2,1)S(1)}) custom-call(bf16[160,1024]{1,0:T(8,128)(2,1)} %wq.1, bf16[64,160]{1,0:T(8,128)(2,1)} %bitcast.7, bf16[64,1024]{1,0:T(8,128)(2,1)} %hq.1, bf16[160,256]{1,0:T(8,128)(2,1)} %wk.1, ...), custom_call_target="tpu_custom_call" | custom-call | tf_op jit(solution)/shard_map/pallas_call | solution.py:390
  50.2 3.3 %shard_map.163 = (bf16[2560,1024]{1,0:T(8,128)(2,1)}, bf16[2560,256]{1,0:T(8,128)(2,1)}, bf16[2560,256]{1,0:T(8,128)(2,1)}, f32[1,1024]{1,0:T(1,128)}, f32[1,256...) custom-call(bf16[2560,1536]{1,0:T(8,128)(2,1)S(1)} %get-tuple-element.19.out, ...), custom_call_target="tpu_custom_call" | custom-call | tf_op jit(solution)/shard_map/pallas_call | solution.py:400
